TPU v7x, 32 devices: a whole 2x2x4 slice. The times are simulated.
32 devices in a mesh: ctx: 16 (over z, y, x), tp: 2 (over core).
Axes of the slice: x: 2, y: 2, z: 4, core: 2. Of those that a mesh axis runs over, the one named last changes fastest.
Arguments:
- hidden_states: bfloat16 [4096, 8192], P('ctx', 'tp'), may hold values from -6 to 6
- queries: bfloat16 [4096, 4096], P('ctx', 'tp')
- key_matrix: bfloat16 [8192, 1024], P('tp'), may hold values from -0.0625 to 0.0625
- value_matrix: bfloat16 [8192, 1024], P('tp'), may hold values from -0.0625 to 0.0625
- stretch_table: int32 [32], replicated, may hold values from 0 to 31, as said below
Outputs:
- attended: bfloat16 [4096, 4096], P('ctx', 'tp')
Inputs may be any that keep to these rules, and one draw needn't show every extreme that they name: `stretch_table`: a permutation of 0 to 31 in which entries 2 i and 2 i + 1 are two stretches c and 31 - c.
All inputs are finite; a program needn't handle non-finite values.
Results may differ from a plain program's by a relative error of at most 0.007.
The roundings to bfloat16 on the way count: a program that leaves them out, or rounds other values in their place, can miss the bound.
Values may be sent and summed in bfloat16 or wider, within the bound.
A program may use at most 256 MiB of HBM per device.

v0:
```python
import functools

import jax
import jax.numpy as jnp
from jax import lax
from jax.experimental import pallas as pl
from jax.experimental.pallas import tpu as pltpu
from jax.sharding import PartitionSpec as P

KEY_VALUE_HEADS = 8
HEAD_SIZE = 128
D = HEAD_SIZE
ROWS = 256
NEG = -1e30
LOG2E = 1.4426950408889634
MESH = pl.DeviceIdType.MESH


def kernel(
    G, R, B, S,
    table, hid_hbm, q_hbm, wk_hbm, wv_hbm, out_hbm,
    hid, w, part_send, part_recv, stage, kv, q_buf, qs, kcat, vcat, acc, mx, ls, o_send,
    hid_sem, w_sem, part_ssem, part_rsem, a2a_ssem, kv_sem, ring_ssem, q_ssem, q_rsem, q_lsem,
    o_ssem, o_rsem, o_lsem,
):
    me = lax.axis_index("ctx")
    tp = lax.axis_index("tp")
    zi = me // G
    ji = me % G
    other = 1 - tp
    up = (zi + 1) % B * G + ji
    down = (zi + B - 1) % B * G + ji
    half_ring = B // 2
    qw = R * D

    order = list(range(1, G)) + [0]

    def fetch(n, k, group):
        col = pl.multiple_of((group * G + (ji + k) % G) * D, D)
        a = pltpu.make_async_copy(wk_hbm.at[:, pl.ds(col, D)], w.at[n, :, pl.ds(0, D)], w_sem.at[n, 0])
        b = pltpu.make_async_copy(wv_hbm.at[:, pl.ds(col, D)], w.at[n, :, pl.ds(D, D)], w_sem.at[n, 1])
        return a, b

    hid_copy = pltpu.make_async_copy(hid_hbm, hid, hid_sem)
    hid_copy.start()
    fetches = []
    for i, k in enumerate(order):
        for which in range(2):
            pair = fetch(2 * i + which, k, other if which == 0 else tp)
            pair[0].start()
            pair[1].start()
            fetches.append(pair)

    barrier = pltpu.get_barrier_semaphore()
    for k in range(1, G):
        pl.semaphore_signal(barrier, inc=1, device_id=(zi * G + (ji + k) % G, tp), device_id_type=MESH)
    pl.semaphore_signal(barrier, inc=1, device_id=(me, other), device_id_type=MESH)
    pl.semaphore_signal(barrier, inc=1, device_id=(up, tp), device_id_type=MESH)
    pl.semaphore_signal(barrier, inc=1, device_id=(down, tp), device_id_type=MESH)
    pl.semaphore_wait(barrier, G + 2)

    def q_copy(k, h):
        p = (ji + k) % G
        return pltpu.make_async_remote_copy(
            src_ref=q_hbm.at[pl.ds(h * S, S), pl.ds(pl.multiple_of(p * qw, qw), qw)],
            dst_ref=q_buf.at[ji, h],
            send_sem=q_ssem.at[k, h],
            recv_sem=q_rsem.at[k, h],
            device_id=(zi * G + p, tp),
            device_id_type=MESH,
        )

    def q_own(h):
        return pltpu.make_async_copy(
            q_hbm.at[pl.ds(h * S, S), pl.ds(pl.multiple_of(ji * qw, qw), qw)], q_buf.at[ji, h], q_lsem.at[h]
        )

    for h in range(2):
        q_own(h).start()
    q_copy(1, 0).start()
    q_copy(G - 1, 0).start()

    def ring_copy(z, j, s, way):
        return pltpu.make_async_remote_copy(
            src_ref=kv.at[z, j],
            dst_ref=kv.at[z, j],
            send_sem=ring_ssem.at[way, s, j],
            recv_sem=kv_sem.at[z, j],
            device_id=(up if way == 0 else down, tp),
            device_id_type=MESH,
        )

    def ring_send(z, j, s, way):
        if s < half_ring - 1:
            ring_copy(z, j, s, way).start()
        else:
            @pl.when((j < G // 2) if way == 0 else (j >= G // 2))
            def _():
                ring_copy(z, j, s, way).start()

    def ring_done(z, j, s, way):
        if s < half_ring - 1:
            ring_copy(z, j, s, way).wait_send()
        else:
            @pl.when((j < G // 2) if way == 0 else (j >= G // 2))
            def _():
                ring_copy(z, j, s, way).wait_send()

    def wait_piece(z, j):
        ring_copy(z, j, 0, 0).wait_recv()

    def part_copy(i):
        return pltpu.make_async_remote_copy(
            src_ref=part_send.at[i],
            dst_ref=part_recv.at[i],
            send_sem=part_ssem.at[i],
            recv_sem=part_rsem.at[i],
            device_id=(me, other),
            device_id_type=MESH,
        )

    def a2a_copy(i, k):
        return pltpu.make_async_remote_copy(
            src_ref=stage.at[i],
            dst_ref=kv.at[zi, ji],
            send_sem=a2a_ssem.at[i],
            recv_sem=kv_sem.at[zi, ji],
            device_id=(zi * G + (ji + k) % G, tp),
            device_id_type=MESH,
        )

    hid_copy.wait()
    for i, k in enumerate(order):
        for n in (2 * i, 2 * i + 1):
            fetches[n][0].wait()
            fetches[n][1].wait()
            term = jnp.dot(hid[...], w[n], preferred_element_type=jnp.float32)
            if n % 2 == 0:
                part_send[i] = term
                part_copy(i).start()
            else:
                part_copy(i).wait_recv()
                both = (term + part_recv[i]).astype(jnp.bfloat16)
                for c in range(2):
                    for h in range(2):
                        block = both[h * S:(h + 1) * S, c * D:(c + 1) * D]
                        if k:
                            stage[i, c, h] = block
                        else:
                            kv[zi, ji, c, h] = block
        if k:
            a2a_copy(i, k).start()
        if i == len(order) - 2:
            for kk in range(1, G):
                for h in range(2):
                    if not (h == 0 and kk in (1, G - 1)):
                        q_copy(kk, h).start()
        if i:
            j = (ji + G - order[i - 1]) % G
            wait_piece(zi, j)
            for way in range(2):
                ring_send(zi, j, 0, way)
        if not k:
            for way in range(2):
                ring_send(zi, ji, 0, way)

    def flipped(z, j):
        return table[2 * (z * G + j)] > table[2 * (z * G + j) + 1]

    def ids(z, j):
        a = table[2 * (z * G + j)]
        b = table[2 * (z * G + j) + 1]
        return jnp.minimum(a, b), jnp.maximum(a, b)

    def sort_queries(j):
        flip = flipped(zi, j)
        first = q_buf[j, 0]
        second = q_buf[j, 1]
        low = jnp.where(flip, second, first)
        high = jnp.where(flip, first, second)
        for r in range(R):
            qs[j, 0, r * S:(r + 1) * S] = low[:, r * D:(r + 1) * D]
            qs[j, 1, r * S:(r + 1) * S] = high[:, r * D:(r + 1) * D]

    for h in range(2):
        q_own(h).wait()
    sort_queries(ji)

    rows_all = R * S
    rows_at = min(ROWS, rows_all)
    scale2 = LOG2E / D**0.5

    def gather_group(z):
        for j in range(G):
            flip = flipped(z, j)
            for c, cat in ((0, kcat), (1, vcat)):
                first = kv[z, j, c, 0]
                second = kv[z, j, c, 1]
                cat[0, j * S:(j + 1) * S] = jnp.where(flip, second, first)
                cat[1, j * S:(j + 1) * S] = jnp.where(flip, first, second)

    def unit(z, jq, h, at, first):
        rows = pl.ds(pl.multiple_of(at * rows_at, rows_at), rows_at)
        qx = qs[jq, h, rows]
        tq = ids(zi, jq)[h]
        row = lax.broadcasted_iota(jnp.int32, (rows_at, S), 0) % S
        col = lax.broadcasted_iota(jnp.int32, (rows_at, S), 1)
        diff = col - row
        pieces = []
        for side in range(h + 1):
            s = lax.dot_general(
                qx, kcat[side], (((1,), (1,)), ((), ())), preferred_element_type=jnp.float32
            )
            for j in range(G):
                block = s[:, j * S:(j + 1) * S]
                if side == h:
                    tk = ids(z, j)[side]
                    block = jnp.where(diff <= (tq - tk) * S, block, jnp.float32(NEG))
                pieces.append(block)
        top = pieces[0]
        for block in pieces[1:]:
            top = jnp.maximum(top, block)
        top = jnp.max(top, axis=1, keepdims=True)
        if first:
            new = jnp.broadcast_to(top, (rows_at, D))
        else:
            old = mx[jq, h, rows]
            new = jnp.maximum(old, top)
        shift = new * scale2
        weights = [jnp.exp2(block * scale2 - shift) for block in pieces]
        total = weights[0]
        for weight in weights[1:]:
            total = total + weight
        value = None
        for side in range(h + 1):
            weight = jnp.concatenate(
                [x.astype(jnp.bfloat16) for x in weights[side * G:(side + 1) * G]], axis=1
            )
            term = jnp.dot(weight, vcat[side], preferred_element_type=jnp.float32)
            value = term if value is None else value + term
        if first:
            acc[jq, h, rows] = value
            ls[jq, h, rows] = total
        else:
            factor = jnp.exp2(old * scale2 - shift)
            acc[jq, h, rows] = acc[jq, h, rows] * factor + value
            ls[jq, h, rows] = ls[jq, h, rows] * factor + total
        mx[jq, h, rows] = new

    def visit_one(z, jq, first):
        def step(at, _):
            for h in range(2):
                unit(z, jq, h, at, first)
            return 0

        lax.fori_loop(0, rows_all // rows_at, step, 0)

    for h in range(2):
        pass
    gather_group(zi)
    visit_one(zi, ji, True)
    for k in range(1, G):
        for h in range(2):
            q_copy(k, h).wait_recv()
        sort_queries((ji + G - k) % G)

    def visit(z, first):
        def step(k, _):
            visit_one(z, (ji + k) % G, first)
            return 0

        lax.fori_loop(1 if first else 0, G, step, 0)

    visit(zi, True)

    for s in range(1, half_ring):
        below = (zi + B - s) % B
        above = (zi + s) % B
        if s < half_ring - 1:
            for j in range(G):
                wait_piece(below, j)
                ring_send(below, j, s, 0)
                wait_piece(above, j)
                ring_send(above, j, s, 1)
        else:
            for j in range(G // 2):
                wait_piece(below, j)
                ring_copy(below, j, s, 0).start()
                wait_piece(above, j + G // 2)
                ring_copy(above, j + G // 2, s, 1).start()
            for j in range(G // 2):
                wait_piece(below, j + G // 2)
        gather_group(below)
        visit(below, False)
        if s == half_ring - 1:
            for j in range(G // 2):
                wait_piece(above, j)
        gather_group(above)
        visit(above, False)

    def o_copy(k):
        p = (ji + k) % G
        return pltpu.make_async_remote_copy(
            src_ref=o_send.at[k],
            dst_ref=out_hbm.at[:, pl.ds(pl.multiple_of(ji * qw, qw), qw)],
            send_sem=o_ssem.at[k],
            recv_sem=o_rsem.at[k],
            device_id=(zi * G + p, tp),
            device_id_type=MESH,
        )

    last = (zi + half_ring) % B
    for j in range(G):
        wait_piece(last, j)
    gather_group(last)

    def finish(k):
        jq = (ji + k) % G
        visit_one(last, jq, False)
        flip = flipped(zi, jq)
        for r in range(R):
            rows = slice(r * S, (r + 1) * S)
            ends = [
                (acc[jq, h, rows] / jnp.sum(ls[jq, h, rows], axis=1, keepdims=True)).astype(jnp.bfloat16)
                for h in range(2)
            ]
            o_send[k, 0:S, r * D:(r + 1) * D] = jnp.where(flip, ends[1], ends[0])
            o_send[k, S:2 * S, r * D:(r + 1) * D] = jnp.where(flip, ends[0], ends[1])

    def finish_step(k, _):
        finish(k)
        o_copy(k).start()
        return 0

    lax.fori_loop(1, G, finish_step, 0)
    finish(0)
    mine = pltpu.make_async_copy(
        o_send.at[0], out_hbm.at[:, pl.ds(pl.multiple_of(ji * qw, qw), qw)], o_lsem
    )
    mine.start()

    for i, k in enumerate(order):
        part_copy(i).wait_send()
        if k:
            a2a_copy(i, k).wait_send()
            for h in range(2):
                q_copy(k, h).wait_send()
    for s in range(half_ring):
        for j in range(G):
            jj = (ji + j) % G
            ring_done((zi + B - s) % B, jj, s, 0)
            ring_done((zi + s) % B, jj, s, 1)
    for k in range(1, G):
        o_copy(k).wait_send()
        o_copy(k).wait_recv()
    mine.wait()


def body(hidden_states, queries, key_matrix, value_matrix, stretch_table):
    tokens, width = hidden_states.shape
    G = KEY_VALUE_HEADS // lax.axis_size("tp")
    ctx = lax.axis_size("ctx")
    B = ctx // G
    S = tokens // 2
    R = queries.shape[1] // (G * D)
    any_ = pl.BlockSpec(memory_space=pl.ANY)
    bf, f32 = jnp.bfloat16, jnp.float32
    dma = pltpu.SemaphoreType.DMA
    return pl.pallas_call(
        functools.partial(kernel, G, R, B, S),
        out_shape=jax.ShapeDtypeStruct(queries.shape, bf),
        in_specs=[pl.BlockSpec(memory_space=pltpu.SMEM)] + [any_] * 4,
        out_specs=any_,
        scratch_shapes=[
            pltpu.VMEM((tokens, width), bf),
            pltpu.VMEM((2 * G, width, 2 * D), bf),
            pltpu.VMEM((G, tokens, 2 * D), f32),
            pltpu.VMEM((G, tokens, 2 * D), f32),
            pltpu.VMEM((G, 2, 2, S, D), bf),
            pltpu.VMEM((B, G, 2, 2, S, D), bf),
            pltpu.VMEM((G, 2, S, R * D), bf),
            pltpu.VMEM((G, 2, R * S, D), bf),
            pltpu.VMEM((2, G * S, D), bf),
            pltpu.VMEM((2, G * S, D), bf),
            pltpu.VMEM((G, 2, R * S, D), f32),
            pltpu.VMEM((G, 2, R * S, D), f32),
            pltpu.VMEM((G, 2, R * S, D), f32),
            pltpu.VMEM((G, tokens, R * D), bf),
            dma,
            dma((2 * G, 2)),
            dma((G,)),
            dma((G,)),
            dma((G,)),
            dma((B, G)),
            dma((2, B // 2, G)),
            dma((G, 2)),
            dma((G, 2)),
            dma((2,)),
            dma((G,)),
            dma((G,)),
            dma,
        ],
        compiler_params=pltpu.CompilerParams(
            collective_id=0, has_side_effects=True, vmem_limit_bytes=60 * 1024 * 1024
        ),
        name="fused",
    )(stretch_table, hidden_states, queries, key_matrix, value_matrix)


def solution(mesh):
    in_specs = (P("ctx", "tp"), P("ctx", "tp"), P("tp", None), P("tp", None), P())
    out_specs = P("ctx", "tp")
    return jax.shard_map(body, mesh=mesh, in_specs=in_specs, out_specs=out_specs, check_vma=False)
```

profile of v0, /device:TPU:1, one launch (start us, length us, event | category | flops | bytes accessed | tf_op | source)
XLA Modules:
  0.0 76.7 jit_solution(3418847899495092372)
XLA Ops:
  0.0 74.4 %fused.1 = bf16[256,2048]{1,0:T(8,128)(2,1)} custom-call(s32[32]{0:T(128)} %table.1, bf16[256,4096]{1,0:T(8,128)(2,1)} %hid_hbm.1, bf16[256,2048]{1,0:T(8,128)(2,1)} %q_hbm.1, bf16[4096,1024]{1,0:T(8,128)(2,1)} %wk_hbm.1, bf16[4096,1024]{1,0:T(8,128)(2,1)} %wv_hbm.1), custom_call_target="tpu_custom_call" | custom-call | tf_op jit(solution)/shard_map/fused/pallas_call | solution.py:369
  74.4 2.3 %copy.7 = bf16[256,2048]{1,0:T(8,128)(2,1)} copy(bf16[256,2048]{1,0:T(8,128)(2,1)} %fused.1) | data formatting | bytes 2097152
where the time goes:
time: 77.9 us; the launch traced here: 76.7 us
  Pallas kernels  74.4 us (96%)
  local copies, waits for them, and re-layouts  2.3 us (3%)
    pallas_call x1, Pallas kernels, body(): pl.pallas_call(functools.partial(kernel, G, R, B, S), out_shape=jax.Shape...  74.4 us
    unnamed x1, local copies, waits for them, and re-layouts  2.3 us

commit v1 on v0

v1 whole, which is shorter than its diff:
```python
import functools

import jax
import jax.numpy as jnp
from jax import lax
from jax.experimental import pallas as pl
from jax.experimental.pallas import tpu as pltpu
from jax.sharding import PartitionSpec as P

KEY_VALUE_HEADS = 8
HEAD_SIZE = 128
D = HEAD_SIZE
ROWS = 256
NEG = -1e30
LOG2E = 1.4426950408889634
MESH = pl.DeviceIdType.MESH


def kernel(
    G, R, NG, S,
    table, hid_hbm, q_hbm, wk_hbm, wv_hbm, out_hbm,
    hid, w, terms, part_recv, stage, kvg, kvo, q_buf, qs, acc, mx, ls, o_send,
    hid_sem, w_sem, part_ssem, part_rsem, a2a_ssem, kvg_sem, kvo_sem, pair_ssem, group_ssem, other_ssem,
    q_ssem, q_rsem, o_ssem, o_rsem,
):
    me = lax.axis_index("ctx")
    c = lax.axis_index("tp")
    j = me % G
    plane = (me // G) % 2
    block = me // (2 * G)
    home = c == plane
    steps = (NG - 1) * G
    qw = R * D

    def peer(r):
        return (j // 2 + r // 2) % 2 * 2 + (j + r) % 2

    def across(r):
        return ((block * 2 + c) * G + peer(r), plane)

    def fetch(n):
        head = (c if n >= G else 1 - c) * G + peer(n % G)
        col = pl.multiple_of(head * D, D)
        a = pltpu.make_async_copy(wk_hbm.at[:, pl.ds(col, D)], w.at[n, :, pl.ds(0, D)], w_sem.at[n, 0])
        b = pltpu.make_async_copy(wv_hbm.at[:, pl.ds(col, D)], w.at[n, :, pl.ds(D, D)], w_sem.at[n, 1])
        return a, b

    hid_copy = pltpu.make_async_copy(hid_hbm, hid, hid_sem)
    hid_copy.start()
    for n in range(2 * G):
        for copy in fetch(n):
            copy.start()

    barrier = pltpu.get_barrier_semaphore()
    pl.semaphore_signal(barrier, inc=1, device_id=(me, 1 - c), device_id_type=MESH)
    for r in range(G):
        pl.semaphore_signal(barrier, inc=1, device_id=across(r), device_id_type=MESH)
    for gi in range(NG - 1):
        there = ((block + gi + 1) % NG * 2 + plane) * G + j
        pl.semaphore_signal(barrier, inc=1, device_id=(there, c), device_id_type=MESH)

    def q_src(r, h):
        return q_hbm.at[pl.ds(h * S, S), pl.ds(pl.multiple_of(peer(r) * qw, qw), qw)]

    def q_copy(r, h):
        return pltpu.make_async_remote_copy(
            src_ref=q_src(r, h),
            dst_ref=q_buf.at[r, h],
            send_sem=q_ssem.at[r, h],
            recv_sem=q_rsem.at[r, h],
            device_id=across(r),
            device_id_type=MESH,
        )

    def q_start(r, h):
        if r:
            q_copy(r, h).start()
        else:
            @pl.when(jnp.logical_not(home))
            def _():
                q_copy(r, h).start()

    @pl.when(home)
    def _():
        for h in range(2):
            pltpu.make_async_copy(q_src(0, h), q_buf.at[0, h], q_rsem.at[0, h]).start()

    def part_copy(r):
        return pltpu.make_async_remote_copy(
            src_ref=terms.at[r],
            dst_ref=part_recv.at[r],
            send_sem=part_ssem.at[r],
            recv_sem=part_rsem.at[r],
            device_id=(me, 1 - c),
            device_id_type=MESH,
        )

    def near(k, r):
        return kvg.at[:, :, pl.ds(pl.multiple_of((k * G + r) * S, S), S)]

    def far(gi, r, k):
        return kvo.at[gi, r, :, :, pl.ds(pl.multiple_of(k * S, S), S)]

    def a2a_copy(r):
        return pltpu.make_async_remote_copy(
            src_ref=stage.at[r],
            dst_ref=near(plane, r),
            send_sem=a2a_ssem.at[r],
            recv_sem=kvg_sem.at[plane, r],
            device_id=across(r),
            device_id_type=MESH,
        )

    def near_wait(k, r):
        pltpu.make_async_copy(near(k, r), near(k, r), kvg_sem.at[k, r]).wait()

    def pair_copy(r):
        return pltpu.make_async_remote_copy(
            src_ref=near(c, r),
            dst_ref=near(c, r),
            send_sem=pair_ssem.at[r],
            recv_sem=kvg_sem.at[c, r],
            device_id=(me, 1 - c),
            device_id_type=MESH,
        )

    def group_copy(gi, r):
        there = ((block + gi + 1) % NG * 2 + plane) * G + j
        return pltpu.make_async_remote_copy(
            src_ref=near(c, r),
            dst_ref=far(NG - 2 - gi, r, c),
            send_sem=group_ssem.at[gi, r],
            recv_sem=kvo_sem.at[NG - 2 - gi, r, c],
            device_id=(there, c),
            device_id_type=MESH,
        )

    def far_wait(s, k):
        gi, r = s // G, s % G
        pltpu.make_async_copy(far(gi, r, k), far(gi, r, k), kvo_sem.at[gi, r, k]).wait()

    def other_copy(s):
        gi, r = s // G, s % G
        return pltpu.make_async_remote_copy(
            src_ref=far(gi, r, c),
            dst_ref=far(gi, r, c),
            send_sem=other_ssem.at[gi, r],
            recv_sem=kvo_sem.at[gi, r, c],
            device_id=(me, 1 - c),
            device_id_type=MESH,
        )

    def pass_on(s):
        far_wait(s, c)
        other_copy(s).start()

    hid_copy.wait()

    def project(n, _):
        for i in range(2):
            half = w.at[n, :, pl.ds(i * D, D)]
            pltpu.make_async_copy(half, half, w_sem.at[n, i]).wait()
        terms[n] = jnp.dot(hid[...], w[n], preferred_element_type=jnp.float32)
        return 0

    lax.fori_loop(0, 2 * G, project, 0)

    pl.semaphore_wait(barrier, 1 + G + NG - 1)
    for r in range(G):
        part_copy(r).start()
    early = ((1, 0), (2, 0))
    for r, h in early:
        q_start(r, h)

    flip = table[2 * me] > table[2 * me + 1]
    for r in range(G):
        part_copy(r).wait_recv()
        both = (terms[G + r] + part_recv[r]).astype(jnp.bfloat16)
        ends = []
        for i in range(2):
            first = both[0:S, i * D:(i + 1) * D]
            second = both[S:2 * S, i * D:(i + 1) * D]
            ends.append((jnp.where(flip, second, first), jnp.where(flip, first, second)))
        if r == 0:
            @pl.when(home)
            def _():
                for i in range(2):
                    for side in range(2):
                        kvg[i, side, pl.ds(pl.multiple_of(c * G * S, S), S)] = ends[i][side]
                pair_copy(0).start()
                for gi in range(NG - 1):
                    group_copy(gi, 0).start()

            @pl.when(jnp.logical_not(home))
            def _():
                for i in range(2):
                    for side in range(2):
                        stage[r, i, side] = ends[i][side]
                a2a_copy(0).start()
        else:
            for i in range(2):
                for side in range(2):
                    stage[r, i, side] = ends[i][side]
            a2a_copy(r).start()
    for r in range(G):
        for h in range(2):
            if (r, h) not in early:
                q_start(r, h)

    for r in range(G):
        def relay():
            near_wait(c, r)
            pair_copy(r).start()
            for gi in range(NG - 1):
                group_copy(gi, r).start()

        if r:
            relay()
        else:
            pl.when(jnp.logical_not(home))(relay)

    def ids(ctx):
        a = table[2 * ctx]
        b = table[2 * ctx + 1]
        return jnp.minimum(a, b), jnp.maximum(a, b)

    def q_ctx(r):
        return (block * 2 + c) * G + peer(r)

    def sort_queries(r):
        for h in range(2):
            q_copy(r, h).wait_recv()
        ctx = q_ctx(r)
        turned = table[2 * ctx] > table[2 * ctx + 1]
        first = q_buf[r, 0]
        second = q_buf[r, 1]
        low = jnp.where(turned, second, first)
        high = jnp.where(turned, first, second)
        for i in range(R):
            qs[r, 0, i * S:(i + 1) * S] = low[:, i * D:(i + 1) * D]
            qs[r, 1, i * S:(i + 1) * S] = high[:, i * D:(i + 1) * D]

    rows_all = R * S
    rows_at = min(ROWS, rows_all)
    scale2 = LOG2E / D**0.5

    def unit(keys, values, places, first, r, h, at):
        rows = pl.ds(pl.multiple_of(at * rows_at, rows_at), rows_at)
        qx = qs[r, h, rows]
        tq = ids(q_ctx(r))[h]
        if first:
            row = lax.broadcasted_iota(jnp.int32, (rows_at, S), 0) % S
            col = lax.broadcasted_iota(jnp.int32, (rows_at, S), 1)
            diff = col - row
        pieces = []
        for side in range(h + 1):
            s = lax.dot_general(
                qx, keys(side), (((1,), (1,)), ((), ())), preferred_element_type=jnp.float32
            )
            for n, place in enumerate(places):
                part = s[:, n * S:(n + 1) * S]
                if side == h:
                    tk = ids(place)[side]
                    if first:
                        part = jnp.where(diff <= (tq - tk) * S, part, jnp.float32(NEG))
                    else:
                        part = part + jnp.where(tk < tq, jnp.float32(0), jnp.float32(NEG))
                pieces.append(part)
        top = pieces[0]
        for part in pieces[1:]:
            top = jnp.maximum(top, part)
        top = jnp.max(top, axis=1, keepdims=True)
        if first:
            new = jnp.broadcast_to(top, (rows_at, D))
        else:
            old = mx[r, h, rows]
            new = jnp.maximum(old, top)
        shift = new * scale2
        weights = [jnp.exp2(part * scale2 - shift) for part in pieces]
        total = weights[0]
        for weight in weights[1:]:
            total = total + weight
        value = None
        count = len(places)
        for side in range(h + 1):
            weight = jnp.concatenate(
                [x.astype(jnp.bfloat16) for x in weights[side * count:(side + 1) * count]], axis=1
            )
            term = jnp.dot(weight, values(side), preferred_element_type=jnp.float32)
            value = term if value is None else value + term
        if first:
            acc[r, h, rows] = value
            ls[r, h, rows] = total
        else:
            factor = jnp.exp2(old * scale2 - shift)
            acc[r, h, rows] = acc[r, h, rows] * factor + value
            ls[r, h, rows] = ls[r, h, rows] * factor + total
        mx[r, h, rows] = new

    def visit_near(r):
        places = [(block * 2 + k) * G + peer(i) for k in range(2) for i in range(G)]

        def step(at, _):
            for h in range(2):
                unit(lambda side: kvg[0, side], lambda side: kvg[1, side], places, True, r, h, at)
            return 0

        lax.fori_loop(0, rows_all // rows_at, step, 0)

    def visit_far(s, r):
        gi, i = s // G, s % G
        places = [((block + gi + 1) % NG * 2 + k) * G + peer(i) for k in range(2)]

        def step(at, _):
            for h in range(2):
                unit(lambda side: kvo[gi, i, 0, side], lambda side: kvo[gi, i, 1, side], places, False, r, h, at)
            return 0

        lax.fori_loop(0, rows_all // rows_at, step, 0)

    for r in range(G):
        near_wait(1 - c, r)

    def near_step(r, _):
        sort_queries(r)
        visit_near(r)

        @pl.when(r < min(2, steps))
        def _():
            pass_on(r)

        return 0

    lax.fori_loop(0, G, near_step, 0)

    def far_step(s, _):
        far_wait(s, 1 - c)

        def one(r, _):
            visit_far(s, r)
            return 0

        lax.fori_loop(0, G, one, 0)

        @pl.when(s >= 1)
        def _():
            pass_on(s + 1)

        return 0

    lax.fori_loop(0, steps - 1, far_step, 0)

    def o_dst():
        return out_hbm.at[:, pl.ds(pl.multiple_of(j * qw, qw), qw)]

    def o_copy(r):
        return pltpu.make_async_remote_copy(
            src_ref=o_send.at[r],
            dst_ref=o_dst(),
            send_sem=o_ssem.at[r],
            recv_sem=o_rsem.at[r],
            device_id=across(r),
            device_id_type=MESH,
        )

    far_wait(steps - 1, 1 - c)

    def finish(i, _):
        r = G - 1 - i
        visit_far(steps - 1, r)
        ctx = q_ctx(r)
        turned = table[2 * ctx] > table[2 * ctx + 1]
        for i in range(R):
            rows = slice(i * S, (i + 1) * S)
            ends = [
                (acc[r, h, rows] / jnp.sum(ls[r, h, rows], axis=1, keepdims=True)).astype(jnp.bfloat16)
                for h in range(2)
            ]
            o_send[r, 0:S, i * D:(i + 1) * D] = jnp.where(turned, ends[1], ends[0])
            o_send[r, S:2 * S, i * D:(i + 1) * D] = jnp.where(turned, ends[0], ends[1])

        @pl.when(jnp.logical_or(r > 0, jnp.logical_not(home)))
        def _():
            o_copy(r).start()

        return 0

    lax.fori_loop(0, G, finish, 0)
    mine = pltpu.make_async_copy(o_send.at[0], o_dst(), o_rsem.at[0])

    @pl.when(home)
    def _():
        mine.start()

    for r in range(G):
        part_copy(r).wait_send()
        pair_copy(r).wait_send()
        for gi in range(NG - 1):
            group_copy(gi, r).wait_send()

        def sent():
            a2a_copy(r).wait_send()
            for h in range(2):
                q_copy(r, h).wait_send()
            o_copy(r).wait_send()

        if r:
            sent()
        else:
            pl.when(jnp.logical_not(home))(sent)
    for s in range(steps):
        other_copy(s).wait_send()
    for r in range(G):
        o_copy(r).wait_recv()


def body(hidden_states, queries, key_matrix, value_matrix, stretch_table):
    tokens, width = hidden_states.shape
    G = KEY_VALUE_HEADS // lax.axis_size("tp")
    NG = lax.axis_size("ctx") // (2 * G)
    S = tokens // 2
    R = queries.shape[1] // (G * D)
    any_ = pl.BlockSpec(memory_space=pl.ANY)
    bf, f32 = jnp.bfloat16, jnp.float32
    dma = pltpu.SemaphoreType.DMA
    return pl.pallas_call(
        functools.partial(kernel, G, R, NG, S),
        out_shape=jax.ShapeDtypeStruct(queries.shape, bf),
        in_specs=[pl.BlockSpec(memory_space=pltpu.SMEM)] + [any_] * 4,
        out_specs=any_,
        scratch_shapes=[
            pltpu.VMEM((tokens, width), bf),
            pltpu.VMEM((2 * G, width, 2 * D), bf),
            pltpu.VMEM((2 * G, tokens, 2 * D), f32),
            pltpu.VMEM((G, tokens, 2 * D), f32),
            pltpu.VMEM((G, 2, 2, S, D), bf),
            pltpu.VMEM((2, 2, 2 * G * S, D), bf),
            pltpu.VMEM((NG - 1, G, 2, 2, 2 * S, D), bf),
            pltpu.VMEM((G, 2, S, R * D), bf),
            pltpu.VMEM((G, 2, R * S, D), bf),
            pltpu.VMEM((G, 2, R * S, D), f32),
            pltpu.VMEM((G, 2, R * S, D), f32),
            pltpu.VMEM((G, 2, R * S, D), f32),
            pltpu.VMEM((G, tokens, R * D), bf),
            dma,
            dma((2 * G, 2)),
            dma((G,)),
            dma((G,)),
            dma((G,)),
            dma((2, G)),
            dma((NG - 1, G, 2)),
            dma((G,)),
            dma((NG - 1, G)),
            dma((NG - 1, G)),
            dma((G, 2)),
            dma((G, 2)),
            dma((G,)),
            dma((G,)),
        ],
        compiler_params=pltpu.CompilerParams(
            collective_id=0, has_side_effects=True, vmem_limit_bytes=60 * 1024 * 1024
        ),
        name="fused",
    )(stretch_table, hidden_states, queries, key_matrix, value_matrix)


def solution(mesh):
    in_specs = (P("ctx", "tp"), P("ctx", "tp"), P("tp", None), P("tp", None), P())
    out_specs = P("ctx", "tp")
    return jax.shard_map(body, mesh=mesh, in_specs=in_specs, out_specs=out_specs, check_vma=False)
```

time: 77.9 us -> 93.5 us (1.20); the launches traced: 76.7 us -> 93.4 us
  Pallas kernels: 74.4 us -> 91.1 us
    pallas_call x1, Pallas kernels: 74.4 us -> 91.1 us  [body(): pl.pallas_call(functools.partial(kernel, G, R, NG, S), out_shape=jax.Shap...]
where the time goes in v1:
time: 93.5 us; the launch traced here: 93.4 us
  Pallas kernels  91.1 us (97%)
  local copies, waits for them, and re-layouts  2.3 us (2%)
    pallas_call x1, Pallas kernels, body(): pl.pallas_call(functools.partial(kernel, G, R, NG, S), out_shape=jax.Shap...  91.1 us
    unnamed x1, local copies, waits for them, and re-layouts  2.3 us

profile of v1, /device:TPU:1, one launch (start us, length us, event | category | flops | bytes accessed | tf_op | source)
XLA Modules:
  0.0 93.4 jit_solution(9728515354054777393)
XLA Ops:
  0.0 91.1 %fused.1 = bf16[256,2048]{1,0:T(8,128)(2,1)} custom-call(s32[32]{0:T(128)} %table.1, bf16[256,4096]{1,0:T(8,128)(2,1)} %hid_hbm.1, bf16[256,2048]{1,0:T(8,128)(2,1)} %q_hbm.1, bf16[4096,1024]{1,0:T(8,128)(2,1)} %wk_hbm.1, bf16[4096,1024]{1,0:T(8,128)(2,1)} %wv_hbm.1), custom_call_target="tpu_custom_call" | custom-call | tf_op jit(solution)/shard_map/fused/pallas_call | solution.py:426
  91.1 2.3 %copy.7 = bf16[256,2048]{1,0:T(8,128)(2,1)} copy(bf16[256,2048]{1,0:T(8,128)(2,1)} %fused.1) | data formatting | bytes 2097152

commit v2 on v1

--- a/solution.py
+++ b/solution.py
@@ -10,8 +10,10 @@
 KEY_VALUE_HEADS = 8
 HEAD_SIZE = 128
 D = HEAD_SIZE
-ROWS = 256
+ROWS = 128
 NEG = -1e30
+AHEAD = 3
+BEFORE = 6
 LOG2E = 1.4426950408889634
 MESH = pl.DeviceIdType.MESH
 
@@ -19,8 +21,8 @@
 def kernel(
     G, R, NG, S,
     table, hid_hbm, q_hbm, wk_hbm, wv_hbm, out_hbm,
-    hid, w, terms, part_recv, stage, kvg, kvo, q_buf, qs, acc, mx, ls, o_send,
-    hid_sem, w_sem, part_ssem, part_rsem, a2a_ssem, kvg_sem, kvo_sem, pair_ssem, group_ssem, other_ssem,
+    hid, w, terms, part_recv, stage, kvg, kvo, q_buf, qs, acc, mx, ls, sc0, tp0, sc1, tp1, o_send,
+    hid_sem, w_sem, part_ssem, part_rsem, a2a_ssem, kvg_sem, kvo_sem, pair_ssem, group_ssem, direct_ssem, other_ssem,
     q_ssem, q_rsem, o_ssem, o_rsem,
 ):
     me = lax.axis_index("ctx")
@@ -29,7 +31,9 @@
     plane = (me // G) % 2
     block = me // (2 * G)
     home = c == plane
+    halves = G // 2
     steps = (NG - 1) * G
+    batches = (NG - 1) * halves
     qw = R * D
 
     def peer(r):
@@ -39,7 +43,7 @@
         return ((block * 2 + c) * G + peer(r), plane)
 
     def fetch(n):
-        head = (c if n >= G else 1 - c) * G + peer(n % G)
+        head = (c + 1 + n // G) % 2 * G + peer(n % G)
         col = pl.multiple_of(head * D, D)
         a = pltpu.make_async_copy(wk_hbm.at[:, pl.ds(col, D)], w.at[n, :, pl.ds(0, D)], w_sem.at[n, 0])
         b = pltpu.make_async_copy(wv_hbm.at[:, pl.ds(col, D)], w.at[n, :, pl.ds(D, D)], w_sem.at[n, 1])
@@ -47,7 +51,7 @@
 
     hid_copy = pltpu.make_async_copy(hid_hbm, hid, hid_sem)
     hid_copy.start()
-    for n in range(2 * G):
+    for n in range(AHEAD):
         for copy in fetch(n):
             copy.start()
 
@@ -58,6 +62,9 @@
     for gi in range(NG - 1):
         there = ((block + gi + 1) % NG * 2 + plane) * G + j
         pl.semaphore_signal(barrier, inc=1, device_id=(there, c), device_id_type=MESH)
+        for r in range(G):
+            there = ((block + gi + 1) % NG * 2 + c) * G + peer(r)
+            pl.semaphore_signal(barrier, inc=1, device_id=(there, plane), device_id_type=MESH)
 
     def q_src(r, h):
         return q_hbm.at[pl.ds(h * S, S), pl.ds(pl.multiple_of(peer(r) * qw, qw), qw)]
@@ -99,7 +106,7 @@
         return kvg.at[:, :, pl.ds(pl.multiple_of((k * G + r) * S, S), S)]
 
     def far(gi, r, k):
-        return kvo.at[gi, r, :, :, pl.ds(pl.multiple_of(k * S, S), S)]
+        return kvo.at[gi, r // 2, :, :, pl.ds(pl.multiple_of((r % 2 * 2 + k) * S, S), S)]
 
     def a2a_copy(r):
         return pltpu.make_async_remote_copy(
@@ -135,6 +142,21 @@
             device_id_type=MESH,
         )
 
+    def facing(gi, p):
+        there = (block + gi + 1) % NG
+        return jnp.where(there > block, p, 1 - p) == 1
+
+    def direct_copy(gi, r):
+        there = ((block + gi + 1) % NG * 2 + c) * G + peer(r)
+        return pltpu.make_async_remote_copy(
+            src_ref=stage.at[r],
+            dst_ref=far(NG - 2 - gi, r, plane),
+            send_sem=direct_ssem.at[gi, r],
+            recv_sem=kvo_sem.at[NG - 2 - gi, r, plane],
+            device_id=(there, plane),
+            device_id_type=MESH,
+        )
+
     def far_wait(s, k):
         gi, r = s // G, s % G
         pltpu.make_async_copy(far(gi, r, k), far(gi, r, k), kvo_sem.at[gi, r, k]).wait()
@@ -160,17 +182,31 @@
         for i in range(2):
             half = w.at[n, :, pl.ds(i * D, D)]
             pltpu.make_async_copy(half, half, w_sem.at[n, i]).wait()
+
+        @pl.when(n + AHEAD < 2 * G)
+        def _():
+            for copy in fetch(n + AHEAD):
+                copy.start()
+
         terms[n] = jnp.dot(hid[...], w[n], preferred_element_type=jnp.float32)
         return 0
 
-    lax.fori_loop(0, 2 * G, project, 0)
-
-    pl.semaphore_wait(barrier, 1 + G + NG - 1)
+    lax.fori_loop(0, BEFORE, project, 0)
+
+    pl.semaphore_wait(barrier, 1 + G + (NG - 1) * (1 + G))
     for r in range(G):
         part_copy(r).start()
     early = ((1, 0), (2, 0))
     for r, h in early:
         q_start(r, h)
+
+    lax.fori_loop(BEFORE, 2 * G, project, 0)
+
+    def direct(r):
+        for gi in range(NG - 1):
+            @pl.when(facing(gi, plane))
+            def _():
+                direct_copy(gi, r).start()
 
     flip = table[2 * me] > table[2 * me + 1]
     for r in range(G):
@@ -197,11 +233,13 @@
                     for side in range(2):
                         stage[r, i, side] = ends[i][side]
                 a2a_copy(0).start()
+                direct(0)
         else:
             for i in range(2):
                 for side in range(2):
                     stage[r, i, side] = ends[i][side]
             a2a_copy(r).start()
+            pl.when(jnp.logical_not(home))(functools.partial(direct, r))
     for r in range(G):
         for h in range(2):
             if (r, h) not in early:
@@ -212,7 +250,9 @@
             near_wait(c, r)
             pair_copy(r).start()
             for gi in range(NG - 1):
-                group_copy(gi, r).start()
+                @pl.when(jnp.logical_or(home, jnp.logical_not(facing(gi, c))))
+                def _():
+                    group_copy(gi, r).start()
 
         if r:
             relay()
@@ -244,88 +284,105 @@
     rows_at = min(ROWS, rows_all)
     scale2 = LOG2E / D**0.5
 
-    def unit(keys, values, places, first, r, h, at):
-        rows = pl.ds(pl.multiple_of(at * rows_at, rows_at), rows_at)
-        qx = qs[r, h, rows]
-        tq = ids(q_ctx(r))[h]
+    def score(to, tops, keys, places, first, r, at):
+        rows = pl.ds(at * rows_at, rows_at)
         if first:
             row = lax.broadcasted_iota(jnp.int32, (rows_at, S), 0) % S
             col = lax.broadcasted_iota(jnp.int32, (rows_at, S), 1)
             diff = col - row
-        pieces = []
-        for side in range(h + 1):
-            s = lax.dot_general(
-                qx, keys(side), (((1,), (1,)), ((), ())), preferred_element_type=jnp.float32
-            )
-            for n, place in enumerate(places):
-                part = s[:, n * S:(n + 1) * S]
-                if side == h:
-                    tk = ids(place)[side]
-                    if first:
-                        part = jnp.where(diff <= (tq - tk) * S, part, jnp.float32(NEG))
-                    else:
-                        part = part + jnp.where(tk < tq, jnp.float32(0), jnp.float32(NEG))
-                pieces.append(part)
-        top = pieces[0]
-        for part in pieces[1:]:
-            top = jnp.maximum(top, part)
-        top = jnp.max(top, axis=1, keepdims=True)
-        if first:
-            new = jnp.broadcast_to(top, (rows_at, D))
-        else:
-            old = mx[r, h, rows]
-            new = jnp.maximum(old, top)
-        shift = new * scale2
-        weights = [jnp.exp2(part * scale2 - shift) for part in pieces]
-        total = weights[0]
-        for weight in weights[1:]:
-            total = total + weight
-        value = None
-        count = len(places)
-        for side in range(h + 1):
-            weight = jnp.concatenate(
-                [x.astype(jnp.bfloat16) for x in weights[side * count:(side + 1) * count]], axis=1
-            )
-            term = jnp.dot(weight, values(side), preferred_element_type=jnp.float32)
-            value = term if value is None else value + term
-        if first:
-            acc[r, h, rows] = value
-            ls[r, h, rows] = total
-        else:
-            factor = jnp.exp2(old * scale2 - shift)
-            acc[r, h, rows] = acc[r, h, rows] * factor + value
-            ls[r, h, rows] = ls[r, h, rows] * factor + total
-        mx[r, h, rows] = new
-
-    def visit_near(r):
+        for h in range(2):
+            qx = qs[r, h, rows]
+            tq = ids(q_ctx(r))[h]
+            top = None
+            for side in range(h + 1):
+                s = lax.dot_general(
+                    qx, keys(side), (((1,), (1,)), ((), ())), preferred_element_type=jnp.float32
+                )
+                for n, place in enumerate(places):
+                    part = s[:, n * S:(n + 1) * S]
+                    if side == h:
+                        tk = ids(place)[side]
+                        if first:
+                            part = jnp.where(diff <= (tq - tk) * S, part, jnp.float32(NEG))
+                        else:
+                            part = part + jnp.where(tk < tq, jnp.float32(0), jnp.float32(NEG))
+                    to[h + side, :, n * S:(n + 1) * S] = part
+                    top = part if top is None else jnp.maximum(top, part)
+            tops[h] = jnp.broadcast_to(jnp.max(top, axis=1, keepdims=True), (rows_at, D))
+
+    def absorb(scores, tops, values, count, first, r, at):
+        rows = pl.ds(at * rows_at, rows_at)
+        for h in range(2):
+            new = tops[h]
+            if not first:
+                old = mx[r, h, rows]
+                new = jnp.maximum(old, new)
+            shift = new * scale2
+            total = None
+            value = None
+            for side in range(h + 1):
+                weights = []
+                for n in range(count):
+                    weight = jnp.exp2(scores[h + side, :, n * S:(n + 1) * S] * scale2 - shift)
+                    total = weight if total is None else total + weight
+                    weights.append(weight.astype(jnp.bfloat16))
+                term = jnp.dot(
+                    jnp.concatenate(weights, axis=1), values(side), preferred_element_type=jnp.float32
+                )
+                value = term if value is None else value + term
+            if first:
+                acc[r, h, rows] = value
+                ls[r, h, rows] = total
+            else:
+                factor = jnp.exp2(old * scale2 - shift)
+                acc[r, h, rows] = acc[r, h, rows] * factor + value
+                ls[r, h, rows] = ls[r, h, rows] * factor + total
+            mx[r, h, rows] = new
+
+    ways = ((sc0, tp0), (sc1, tp1))
+    blocks = rows_all // rows_at
+
+    def near_score(r, at):
         places = [(block * 2 + k) * G + peer(i) for k in range(2) for i in range(G)]
-
-        def step(at, _):
-            for h in range(2):
-                unit(lambda side: kvg[0, side], lambda side: kvg[1, side], places, True, r, h, at)
-            return 0
-
-        lax.fori_loop(0, rows_all // rows_at, step, 0)
-
-    def visit_far(s, r):
-        gi, i = s // G, s % G
-        places = [((block + gi + 1) % NG * 2 + k) * G + peer(i) for k in range(2)]
-
-        def step(at, _):
-            for h in range(2):
-                unit(lambda side: kvo[gi, i, 0, side], lambda side: kvo[gi, i, 1, side], places, False, r, h, at)
-            return 0
-
-        lax.fori_loop(0, rows_all // rows_at, step, 0)
+        score(*ways[at % 2], lambda side: kvg[0, side], places, True, r, at)
+
+    def near_absorb(r, at):
+        absorb(*ways[at % 2], lambda side: kvg[1, side], 2 * G, True, r, at)
+
+    def far_score(b, r, at):
+        gi, i = b // halves, b % halves
+        there = (block + gi + 1) % NG * 2
+        places = [(there + k) * G + peer(2 * i + a) for a in range(2) for k in range(2)]
+        score(*ways[at % 2], lambda side: kvo[gi, i, 0, side], places, False, r, at)
+
+    def far_absorb(b, r, at):
+        gi, i = b // halves, b % halves
+        absorb(*ways[at % 2], lambda side: kvo[gi, i, 1, side], 4, False, r, at)
+
+    def through(score_at, absorb_at, r, then):
+        for at in range(blocks):
+            if at + 1 < blocks:
+                score_at(r, at + 1)
+            else:
+                score_at(then, 0)
+            absorb_at(r, at)
 
     for r in range(G):
         near_wait(1 - c, r)
 
+    sort_queries(0)
+    near_score(0, 0)
+
     def near_step(r, _):
-        sort_queries(r)
-        visit_near(r)
-
-        @pl.when(r < min(2, steps))
+        then = (r + 1) % G
+
+        @pl.when(r + 1 < G)
+        def _():
+            sort_queries(then)
+
+        through(near_score, near_absorb, r, then)
+
+        @pl.when(r < 2)
         def _():
             pass_on(r)
 
@@ -333,22 +390,21 @@
 
     lax.fori_loop(0, G, near_step, 0)
 
-    def far_step(s, _):
-        far_wait(s, 1 - c)
+    def far_step(b, _):
+        for a in range(2):
+            far_wait(2 * b + a, 1 - c)
+        far_score(b, 0, 0)
 
         def one(r, _):
-            visit_far(s, r)
+            through(functools.partial(far_score, b), functools.partial(far_absorb, b), r, (r + 1) % G)
             return 0
 
         lax.fori_loop(0, G, one, 0)
-
-        @pl.when(s >= 1)
-        def _():
-            pass_on(s + 1)
-
+        for a in range(2):
+            pass_on(2 * b + 2 + a)
         return 0
 
-    lax.fori_loop(0, steps - 1, far_step, 0)
+    lax.fori_loop(0, batches - 1, far_step, 0)
 
     def o_dst():
         return out_hbm.at[:, pl.ds(pl.multiple_of(j * qw, qw), qw)]
@@ -363,11 +419,14 @@
             device_id_type=MESH,
         )
 
-    far_wait(steps - 1, 1 - c)
+    for a in range(2):
+        far_wait(steps - 2 + a, 1 - c)
+    last = batches - 1
+    far_score(last, G - 1, 0)
 
     def finish(i, _):
         r = G - 1 - i
-        visit_far(steps - 1, r)
+        through(functools.partial(far_score, last), functools.partial(far_absorb, last), r, (r + G - 1) % G)
         ctx = q_ctx(r)
         turned = table[2 * ctx] > table[2 * ctx + 1]
         for i in range(R):
@@ -396,7 +455,13 @@
         part_copy(r).wait_send()
         pair_copy(r).wait_send()
         for gi in range(NG - 1):
-            group_copy(gi, r).wait_send()
+            @pl.when(jnp.logical_or(home, jnp.logical_not(facing(gi, c))))
+            def _():
+                group_copy(gi, r).wait_send()
+
+            @pl.when(jnp.logical_and(facing(gi, plane), jnp.logical_not(home)))
+            def _():
+                direct_copy(gi, r).wait_send()
 
         def sent():
             a2a_copy(r).wait_send()
@@ -420,6 +485,7 @@
     NG = lax.axis_size("ctx") // (2 * G)
     S = tokens // 2
     R = queries.shape[1] // (G * D)
+    rows_at = min(ROWS, R * S)
     any_ = pl.BlockSpec(memory_space=pl.ANY)
     bf, f32 = jnp.bfloat16, jnp.float32
     dma = pltpu.SemaphoreType.DMA
@@ -435,12 +501,16 @@
             pltpu.VMEM((G, tokens, 2 * D), f32),
             pltpu.VMEM((G, 2, 2, S, D), bf),
             pltpu.VMEM((2, 2, 2 * G * S, D), bf),
-            pltpu.VMEM((NG - 1, G, 2, 2, 2 * S, D), bf),
+            pltpu.VMEM((NG - 1, G // 2, 2, 2, 4 * S, D), bf),
             pltpu.VMEM((G, 2, S, R * D), bf),
             pltpu.VMEM((G, 2, R * S, D), bf),
             pltpu.VMEM((G, 2, R * S, D), f32),
             pltpu.VMEM((G, 2, R * S, D), f32),
             pltpu.VMEM((G, 2, R * S, D), f32),
+            pltpu.VMEM((3, rows_at, 2 * G * S), f32),
+            pltpu.VMEM((2, rows_at, D), f32),
+            pltpu.VMEM((3, rows_at, 2 * G * S), f32),
+            pltpu.VMEM((2, rows_at, D), f32),
             pltpu.VMEM((G, tokens, R * D), bf),
             dma,
             dma((2 * G, 2)),
@@ -450,6 +520,7 @@
             dma((2, G)),
             dma((NG - 1, G, 2)),
             dma((G,)),
+            dma((NG - 1, G)),
             dma((NG - 1, G)),
             dma((NG - 1, G)),
             dma((G, 2)),

time: 93.5 us -> 68.9 us (0.74)
  Pallas kernels: 91.1 us -> 66.4 us
    pallas_call x1, Pallas kernels: 91.1 us -> 66.4 us  [body(): pl.pallas_call(functools.partial(kernel, G, R, NG, S), out_shape=jax.Shap...]
where the time goes in v2:
time: 68.9 us; the launch traced here: 68.7 us
  Pallas kernels  66.4 us (96%)
  local copies, waits for them, and re-layouts  2.3 us (3%)
    pallas_call x1, Pallas kernels, body(): pl.pallas_call(functools.partial(kernel, G, R, NG, S), out_shape=jax.Shap...  66.4 us
    unnamed x1, local copies, waits for them, and re-layouts  2.3 us

profile of v2, /device:TPU:1, one launch (start us, length us, event | category | flops | bytes accessed | tf_op | source)
XLA Modules:
  0.0 68.7 jit_solution(14932116859986831100)
XLA Ops:
  0.0 66.4 %fused.1 = bf16[256,2048]{1,0:T(8,128)(2,1)} custom-call(s32[32]{0:T(128)} %table.1, bf16[256,4096]{1,0:T(8,128)(2,1)} %hid_hbm.1, bf16[256,2048]{1,0:T(8,128)(2,1)} %q_hbm.1, bf16[4096,1024]{1,0:T(8,128)(2,1)} %wk_hbm.1, bf16[4096,1024]{1,0:T(8,128)(2,1)} %wv_hbm.1), custom_call_target="tpu_custom_call" | custom-call | tf_op jit(solution)/shard_map/fused/pallas_call | solution.py:492
  66.4 2.3 %copy.7 = bf16[256,2048]{1,0:T(8,128)(2,1)} copy(bf16[256,2048]{1,0:T(8,128)(2,1)} %fused.1) | data formatting | bytes 2097152

commit v3 on v2

--- a/solution.py
+++ b/solution.py
@@ -13,7 +13,7 @@
 ROWS = 128
 NEG = -1e30
 AHEAD = 3
-BEFORE = 6
+BEFORE = 4
 LOG2E = 1.4426950408889634
 MESH = pl.DeviceIdType.MESH
 
@@ -196,7 +196,7 @@
     pl.semaphore_wait(barrier, 1 + G + (NG - 1) * (1 + G))
     for r in range(G):
         part_copy(r).start()
-    early = ((1, 0), (2, 0))
+    early = ((0, 0), (0, 1), (1, 0), (1, 1))
     for r, h in early:
         q_start(r, h)
 
@@ -342,12 +342,14 @@
     ways = ((sc0, tp0), (sc1, tp1))
     blocks = rows_all // rows_at
 
-    def near_score(r, at):
-        places = [(block * 2 + k) * G + peer(i) for k in range(2) for i in range(G)]
-        score(*ways[at % 2], lambda side: kvg[0, side], places, True, r, at)
-
-    def near_absorb(r, at):
-        absorb(*ways[at % 2], lambda side: kvg[1, side], 2 * G, True, r, at)
+    def near_score(k, own, r, at):
+        places = [(block * 2 + k) * G + peer(i) for i in range(G)]
+        at_k = pl.ds(pl.multiple_of(k * G * S, G * S), G * S)
+        score(*ways[at % 2], lambda side: kvg[0, side, at_k], places, own, r, at)
+
+    def near_absorb(k, own, r, at):
+        at_k = pl.ds(pl.multiple_of(k * G * S, G * S), G * S)
+        absorb(*ways[at % 2], lambda side: kvg[1, side, at_k], G, own, r, at)
 
     def far_score(b, r, at):
         gi, i = b // halves, b % halves
@@ -364,23 +366,36 @@
             if at + 1 < blocks:
                 score_at(r, at + 1)
             else:
-                score_at(then, 0)
+                then()
             absorb_at(r, at)
 
-    for r in range(G):
-        near_wait(1 - c, r)
-
     sort_queries(0)
-    near_score(0, 0)
+    near_score(c, True, 0, 0)
 
     def near_step(r, _):
-        then = (r + 1) % G
+        after = (r + 1) % G
 
         @pl.when(r + 1 < G)
         def _():
-            sort_queries(then)
-
-        through(near_score, near_absorb, r, then)
+            sort_queries(after)
+
+        for at in range(blocks - 1):
+            near_score(c, True, r, at + 1)
+            near_absorb(c, True, r, at)
+
+        @pl.when(r == 0)
+        def _():
+            for i in range(G):
+                near_wait(1 - c, i)
+
+        near_score(1 - c, False, r, 0)
+        near_absorb(c, True, r, blocks - 1)
+        through(
+            functools.partial(near_score, 1 - c, False),
+            functools.partial(near_absorb, 1 - c, False),
+            r,
+            functools.partial(near_score, c, True, after, 0),
+        )
 
         @pl.when(r < 2)
         def _():
@@ -389,6 +404,7 @@
         return 0
 
     lax.fori_loop(0, G, near_step, 0)
+    pass_on(2)
 
     def far_step(b, _):
         for a in range(2):
@@ -396,12 +412,25 @@
         far_score(b, 0, 0)
 
         def one(r, _):
-            through(functools.partial(far_score, b), functools.partial(far_absorb, b), r, (r + 1) % G)
+            through(
+                functools.partial(far_score, b),
+                functools.partial(far_absorb, b),
+                r,
+                functools.partial(far_score, b, (r + 1) % G, 0),
+            )
+
+            @pl.when(r == 2)
+            def _():
+                pass_on(2 * b + 3)
+
             return 0
 
         lax.fori_loop(0, G, one, 0)
-        for a in range(2):
-            pass_on(2 * b + 2 + a)
+
+        @pl.when(2 * b + 4 < steps)
+        def _():
+            pass_on(2 * b + 4)
+
         return 0
 
     lax.fori_loop(0, batches - 1, far_step, 0)
@@ -426,7 +455,12 @@
 
     def finish(i, _):
         r = G - 1 - i
-        through(functools.partial(far_score, last), functools.partial(far_absorb, last), r, (r + G - 1) % G)
+        through(
+            functools.partial(far_score, last),
+            functools.partial(far_absorb, last),
+            r,
+            functools.partial(far_score, last, (r + G - 1) % G, 0),
+        )
         ctx = q_ctx(r)
         turned = table[2 * ctx] > table[2 * ctx + 1]
         for i in range(R):
@@ -507,9 +541,9 @@
             pltpu.VMEM((G, 2, R * S, D), f32),
             pltpu.VMEM((G, 2, R * S, D), f32),
             pltpu.VMEM((G, 2, R * S, D), f32),
-            pltpu.VMEM((3, rows_at, 2 * G * S), f32),
+            pltpu.VMEM((3, rows_at, G * S), f32),
             pltpu.VMEM((2, rows_at, D), f32),
-            pltpu.VMEM((3, rows_at, 2 * G * S), f32),
+            pltpu.VMEM((3, rows_at, G * S), f32),
             pltpu.VMEM((2, rows_at, D), f32),
             pltpu.VMEM((G, tokens, R * D), bf),
             dma,

time: 68.9 us -> 68 us (0.987)
  Pallas kernels: 66.4 us -> 65.1 us
    pallas_call x1, Pallas kernels: 66.4 us -> 65.1 us  [body(): pl.pallas_call(functools.partial(kernel, G, R, NG, S), out_shape=jax.Shap...]
where the time goes in v3:
time: 68 us; the launch traced here: 67.4 us
  Pallas kernels  65.1 us (96%)
  local copies, waits for them, and re-layouts  2.3 us (3%)
    pallas_call x1, Pallas kernels, body(): pl.pallas_call(functools.partial(kernel, G, R, NG, S), out_shape=jax.Shap...  65.1 us
    unnamed x1, local copies, waits for them, and re-layouts  2.3 us

profile of v3, /device:TPU:1, one launch (start us, length us, event | category | flops | bytes accessed | tf_op | source)
XLA Modules:
  0.0 67.4 jit_solution(460085630644683197)
XLA Ops:
  0.0 65.1 %fused.1 = bf16[256,2048]{1,0:T(8,128)(2,1)} custom-call(s32[32]{0:T(128)} %table.1, bf16[256,4096]{1,0:T(8,128)(2,1)} %hid_hbm.1, bf16[256,2048]{1,0:T(8,128)(2,1)} %q_hbm.1, bf16[4096,1024]{1,0:T(8,128)(2,1)} %wk_hbm.1, bf16[4096,1024]{1,0:T(8,128)(2,1)} %wv_hbm.1), custom_call_target="tpu_custom_call" | custom-call | tf_op jit(solution)/shard_map/fused/pallas_call | solution.py:526
  65.1 2.3 %copy.7 = bf16[256,2048]{1,0:T(8,128)(2,1)} copy(bf16[256,2048]{1,0:T(8,128)(2,1)} %fused.1) | data formatting | bytes 2097152
